TPU v7x, 32 devices: a whole 2x2x4 slice. The times are simulated.
32 devices in a mesh: energy: 8 (over y, x, core), mom: 4 (over z).
Axes of the slice: x: 2, y: 2, z: 4, core: 2. Of those that a mesh axis runs over, the one named last changes fastest.
Arguments:
- lesser: float32 [4, 8, 4, 4, 2, 128, 128], P(None, 'energy', 'mom'), as said below
- greater: float32 [4, 8, 4, 4, 2, 128, 128], P(None, 'energy', 'mom'), as said below
- hamiltonian: float32 [4, 4, 2, 128, 128], P('mom'), as said below
- coupling: float32 [4, 2, 128, 128], P('mom'), may hold values from -0.25 to 0.25
- shift: int32 [1], replicated, may hold values from 1 to 7
- phonon_weight: float32 [2], replicated, may hold values from 0.1 to 0.5
Outputs:
- lesser_next: float32 [4, 8, 4, 4, 2, 128, 128], P(None, 'energy', 'mom')
- greater_next: float32 [4, 8, 4, 4, 2, 128, 128], P(None, 'energy', 'mom')
- current: float32 [], replicated
Inputs may be any that keep to these rules, and one draw needn't show every extreme that they name: `lesser`: in each block the complex matrix is i times a Hermitian positive definite matrix. `greater`: in each block the complex matrix is -i times a Hermitian positive definite matrix. `hamiltonian`: each block is Hermitian: real part symmetric, imaginary part antisymmetric.
All inputs are finite; a program needn't handle non-finite values.
Results may differ from a plain program's by a relative error of at most 0.0001.
Values sent between devices are 32-bit elements; how exact they have to be, the bound alone decides.
A program may use at most 128 MiB of HBM per device.

v0:
```python
import jax
import jax.numpy as jnp
from jax import lax
from jax.sharding import PartitionSpec as P

SMAX = 7


broaden = 0.2
contact_rate = 0.5
left_level = 0.3
right_level = -0.3
thermal = 0.1
band_edge = 2.0
precise = lax.Precision.HIGHEST


def shifted(array, axis, by):
    size = lax.axis_size(axis)
    return lax.ppermute(array, axis, [(i, (i + by) % size) for i in range(size)])


def product(left, right):
    return jnp.einsum("...ij,...jk->...ik", left, right, precision=precise)


def cmul(left, right):
    return (
        product(left[0], right[0]) - product(left[1], right[1]),
        product(left[0], right[1]) + product(left[1], right[0]),
    )


def dagger(value):
    return (jnp.swapaxes(value[0], -1, -2), -jnp.swapaxes(value[1], -1, -2))


def sandwich(outer, inner):
    return cmul(cmul(outer, inner), dagger(outer))


def invert(matrix):
    real, imag = matrix
    width = real.shape[-1]
    kernel = jnp.concatenate(
        [jnp.concatenate([real, -imag], -1), jnp.concatenate([imag, real], -1)], -2
    )
    normal = product(jnp.swapaxes(kernel, -1, -2), kernel)
    lower = jnp.linalg.cholesky(normal)
    rhs = jnp.concatenate([jnp.swapaxes(real, -1, -2), -jnp.swapaxes(imag, -1, -2)], -2)
    middle = jax.scipy.linalg.solve_triangular(lower, rhs, lower=True)
    result = jax.scipy.linalg.solve_triangular(lower, middle, lower=True, trans=1)
    guess = (result[..., :width, :], result[..., width:, :])
    check = cmul(matrix, guess)
    eye = jnp.eye(width, dtype=jnp.float32)
    return cmul(guess, (2.0 * eye - check[0], -check[1]))


def transport(energy, hamiltonian, coupling, sig_less, sig_great):
    slabs = hamiltonian.shape[1]
    width = hamiltonian.shape[-1]
    eye = jnp.eye(width, dtype=jnp.float32)
    level = energy[:, None, None]
    hop = (coupling[:, 0], coupling[:, 1])
    hop_back = dagger(hop)
    fill_left = jax.nn.sigmoid((left_level - energy) / thermal)
    fill_right = jax.nn.sigmoid((right_level - energy) / thermal)
    forward_r = []
    forward_l = []
    for slab in range(slabs):
        less_re = sig_less[:, slab, 0]
        less_im = sig_less[:, slab, 1]
        system_re = level * eye - hamiltonian[:, slab, 0] - 0.5 * (sig_great[:, slab, 0] - less_re)
        system_im = (
            broaden * eye - hamiltonian[:, slab, 1] - 0.5 * (sig_great[:, slab, 1] - less_im)
        )
        inject_re = less_re
        inject_im = less_im
        if slab == 0 or slab == slabs - 1:
            filling = fill_left if slab == 0 else fill_right
            system_im = system_im + contact_rate * eye
            inject_im = inject_im + 2.0 * contact_rate * filling[:, None, None] * eye
        if slab > 0:
            folded = sandwich(hop, forward_r[-1])
            system_re = system_re - folded[0]
            system_im = system_im - folded[1]
            carried = sandwich(hop, forward_l[-1])
            inject_re = inject_re + carried[0]
            inject_im = inject_im + carried[1]
        green = invert((system_re, system_im))
        forward_r.append(green)
        forward_l.append(sandwich(green, (inject_re, inject_im)))
    full_r = forward_r[-1]
    full_l = forward_l[-1]
    outs_r = [full_r]
    outs_l = [full_l]
    for slab in range(slabs - 2, -1, -1):
        green = forward_r[slab]
        green_l = forward_l[slab]
        lead = cmul(green, hop_back)
        spread = cmul(lead, full_r)
        tail = cmul(hop, green)
        extra = cmul(spread, tail)
        new_r = (green[0] + extra[0], green[1] + extra[1])
        cross = cmul(spread, cmul(hop, green_l))
        inner = sandwich(lead, full_l)
        cross_d = dagger(cross)
        new_l = (
            green_l[0] + inner[0] + cross[0] - cross_d[0],
            green_l[1] + inner[1] + cross[1] - cross_d[1],
        )
        full_r = new_r
        full_l = new_l
        outs_r.insert(0, full_r)
        outs_l.insert(0, full_l)
    less_blocks = jnp.stack([jnp.stack([value[0], value[1]], 1) for value in outs_l], 1)
    great_blocks = jnp.stack(
        [
            jnp.stack(
                [
                    outs_l[k][0] + outs_r[k][0] - jnp.swapaxes(outs_r[k][0], -1, -2),
                    outs_l[k][1] + outs_r[k][1] + jnp.swapaxes(outs_r[k][1], -1, -2),
                ],
                1,
            )
            for k in range(slabs)
        ],
        1,
    )
    great_trace = jnp.trace(great_blocks[:, 0, 1], axis1=-2, axis2=-1)
    less_trace = jnp.trace(less_blocks[:, 0, 1], axis1=-2, axis2=-1)
    flowing = -(
        2.0 * contact_rate * fill_left * great_trace
        + 2.0 * contact_rate * (1.0 - fill_left) * less_trace
    )
    return (less_blocks, great_blocks, flowing)


def displaced(field, amount):
    count = field.shape[1]
    padded = jnp.concatenate([jnp.zeros_like(field), field, jnp.zeros_like(field)], 1)
    start = count + jnp.clip(amount, -count, count)
    return lax.dynamic_slice_in_dim(padded, start, count, 1)


def onward(field, upward):
    blank = jnp.zeros_like(field[:, :1])
    if upward:
        return jnp.concatenate([field[:, 1:], blank], 1)
    return jnp.concatenate([blank, field[:, :-1]], 1)


def fetched(stacked, amount, upward):
    n_energy = lax.axis_size("energy")
    here = lax.axis_index("energy")
    whole_turns = amount // n_energy
    remainder = amount % n_energy
    direction = 1 if upward else -1
    stacked = displaced(stacked, direction * whole_turns)
    level = 1
    while level <= min(SMAX, n_energy - 1):
        if upward:
            arrived = shifted(stacked, "energy", -level)
            wrapped = here + level >= n_energy
        else:
            arrived = shifted(stacked, "energy", level)
            wrapped = here - level < 0
        arrived = jnp.where(wrapped, onward(arrived, upward), arrived)
        taken = remainder // level % 2 == 1
        stacked = jnp.where(taken, arrived, stacked)
        level = level * 2
    return stacked


def shards(lesser, greater, hamiltonian, coupling, shift, phonon_weight):
    n_energy = lax.axis_size("energy")
    n_mom = lax.axis_size("mom")
    here = lax.axis_index("energy")
    per_dev = lesser.shape[0]
    total = per_dev * n_energy
    both = jnp.stack([lesser[:, 0, 0], greater[:, 0, 0]], 0)
    amount = shift[0]
    emission = phonon_weight[0]
    absorption = phonon_weight[1]
    summed = lax.psum_scatter(both, "mom", scatter_dimension=2, tiled=True)
    mean = summed / n_mom
    upper = fetched(mean, amount, True)
    beneath = fetched(mean, amount, False)
    share_less = emission * upper[0] + absorption * beneath[0]
    share_great = emission * beneath[1] + absorption * upper[1]
    sig_both = lax.all_gather(jnp.stack([share_less, share_great], 0), "mom", axis=2, tiled=True)
    sig_less = sig_both[0]
    sig_great = sig_both[1]
    grid = (jnp.arange(per_dev) * n_energy + here).astype(jnp.float32)
    energy = (grid + 0.5) * (2.0 * band_edge / total) - band_edge
    ham_wide = jnp.broadcast_to(hamiltonian, (per_dev,) + hamiltonian.shape[1:])
    hop_wide = jnp.broadcast_to(coupling, (per_dev,) + coupling.shape[1:])
    less_new, great_new, flowing = transport(energy, ham_wide, hop_wide, sig_less, sig_great)
    partial_flow = jnp.sum(flowing) * (2.0 * band_edge / total)
    current = lax.psum(partial_flow, ("energy", "mom"))
    return (less_new[:, None, None], great_new[:, None, None], current)


def solution(mesh):
    in_specs = (
        P(None, "energy", "mom", None, None, None, None),
        P(None, "energy", "mom", None, None, None, None),
        P("mom", None, None, None, None),
        P("mom", None, None, None),
        P(),
        P(),
    )
    out_specs = (
        P(None, "energy", "mom", None, None, None, None),
        P(None, "energy", "mom", None, None, None, None),
        P(),
    )
    return jax.shard_map(shards, mesh=mesh, in_specs=in_specs, out_specs=out_specs, check_vma=False)
```

profile of v0, /device:TPU:0, one launch (start us, length us, event | category | flops | bytes accessed | tf_op | source)
XLA Modules:
  0.0 1578.9 jit_solution(17530587482474955595)
XLA Ops:
  13.3 156.5 %all-reduce.10.cloned.1.call-done = f32[2,4,4,2,128,128]{5,4,1,3,2,0:T(8,128)} async-done(((f32[2,4,4,2,128,128]{5,4,1,3,2,0:T(8,128)}), f32[2,4,4,2,128,128]{5,4,1,3,2,0:T(8,128)}) %all-reduce.10.cloned.1.call-update) | async-done | bytes 4194320
  175.2 21.9 %collective-permute-done.3 = f32[2,4,1,2,128,128]{5,4,1,3,2,0:T(8,128)S(1)} collective-permute-done((f32[2,4,1,2,128,128]{5,4,1,3,2,0:T(8,128)S(1)}, f32[2,4,1,2,128,128]{5,4,1,3,2,0:T(8,128)S(1)}, u32[]{:S(2)}, u32[]{:S(2)}) %collective-permute-start.3) | collective-permute-done | bytes 1048608 | tf_op jit(solution)/shard_map/ppermute | solution.py:20
  204.1 21.4 %collective-permute-done.4 = f32[2,4,1,2,128,128]{5,4,1,3,2,0:T(8,128)} collective-permute-done((f32[2,4,1,2,128,128]{5,4,1,3,2,0:T(8,128)S(1)}, f32[2,4,1,2,128,128]{5,4,1,3,2,0:T(8,128)}, u32[]{:S(2)}, u32[]{:S(2)}) %collective-permute-start.4) | collective-permute-done | bytes 1048608 | tf_op jit(solution)/shard_map/ppermute | solution.py:20
  231.8 14.6 collective-permute-done.1
  251.5 20.8 %collective-permute-done.2 = f32[2,4,1,2,128,128]{5,4,1,3,2,0:T(8,128)S(1)} collective-permute-done((f32[2,4,1,2,128,128]{5,4,1,3,2,0:T(8,128)S(1)}, f32[2,4,1,2,128,128]{5,4,1,3,2,0:T(8,128)S(1)}, u32[]{:S(2)}, u32[]{:S(2)}) %collective-permute-start.2) | collective-permute-done | bytes 1048608 | tf_op jit(solution)/shard_map/ppermute | solution.py:20
  278.8 96.6 %all-gather.2.cloned.1.call-done = f32[2,4,4,2,128,128]{5,4,1,3,2,0:T(8,128)} async-done(((f32[2,4,1,2,128,128]{5,4,1,3,2,0:T(8,128)}), f32[2,4,4,2,128,128]{5,4,1,3,2,0:T(8,128)}) %all-gather.2.cloned.1.call-update) | async-done | bytes 4194320 | tf_op jit(solution)/shard_map/all_gather | solution.py:191
  383.3 47.1 %custom-call.31 = f32[4,128,128]{2,1,0:T(8,128)S(1)} custom-call(f32[4,128,128]{2,1,0:T(8,128)S(1)} %cholesky.350), custom_call_target="Cholesky" | custom-call | tf_op jit(solution)/shard_map/jit(cholesky)/cholesky | solution.py:49
  430.5 39.3 %custom-call.32 = f32[4,1,128,128]{2,3,1,0:T(8,128)S(1)} custom-call(f32[4,1,128,128]{3,2,1,0:T(8,128)S(1)} %select_bitcast_fusion.3), custom_call_target="InvertDiagBlocksLowerTriangular" | custom-call | tf_op jit(solution)/shard_map/jit(cholesky)/cholesky | solution.py:49
  472.8 46.9 %custom-call.33 = f32[4,128,128]{2,1,0:T(8,128)S(1)} custom-call(f32[4,128,128]{2,1,0:T(8,128)S(1)} %convolution_subtract_fusion.57), custom_call_target="Cholesky" | custom-call | tf_op jit(solution)/shard_map/jit(cholesky)/cholesky | solution.py:49
  525.8 79.0 %custom-call.35 = f32[4,2,128,128]{2,3,1,0:T(8,128)S(1)} custom-call(f32[4,2,128,128]{3,2,1,0:T(8,128)S(1)} %bitcast.805), custom_call_target="InvertDiagBlocksLowerTriangular" | custom-call | tf_op jit(solution)/shard_map/jit(_solve_triangular)/vmap()/triangular_solve | solution.py:52
  622.4 46.9 %custom-call.36 = f32[4,128,128]{2,1,0:T(8,128)S(1)} custom-call(f32[4,128,128]{2,1,0:T(8,128)S(1)} %cholesky.353), custom_call_target="Cholesky" | custom-call | tf_op jit(solution)/shard_map/jit(cholesky)/cholesky | solution.py:49
  670.2 39.3 %custom-call.37 = f32[4,1,128,128]{2,3,1,0:T(8,128)S(1)} custom-call(f32[4,1,128,128]{3,2,1,0:T(8,128)S(1)} %select_bitcast_fusion.2), custom_call_target="InvertDiagBlocksLowerTriangular" | custom-call | tf_op jit(solution)/shard_map/jit(cholesky)/cholesky | solution.py:49
  712.5 46.9 %custom-call.38 = f32[4,128,128]{2,1,0:T(8,128)S(1)} custom-call(f32[4,128,128]{2,1,0:T(8,128)S(1)} %convolution_subtract_fusion.47), custom_call_target="Cholesky" | custom-call | tf_op jit(solution)/shard_map/jit(cholesky)/cholesky | solution.py:49
  765.4 79.6 %custom-call.40 = f32[4,2,128,128]{2,3,1,0:T(8,128)} custom-call(f32[4,2,128,128]{3,2,1,0:T(8,128)S(1)} %bitcast.806), custom_call_target="InvertDiagBlocksLowerTriangular" | custom-call | tf_op jit(solution)/shard_map/jit(_solve_triangular)/vmap()/triangular_solve | solution.py:52
  867.5 46.9 %custom-call.41 = f32[4,128,128]{2,1,0:T(8,128)S(1)} custom-call(f32[4,128,128]{2,1,0:T(8,128)S(1)} %cholesky.356), custom_call_target="Cholesky" | custom-call | tf_op jit(solution)/shard_map/jit(cholesky)/cholesky | solution.py:49
  915.3 40.7 %custom-call.42 = f32[4,1,128,128]{2,3,1,0:T(8,128)} custom-call(f32[4,1,128,128]{3,2,1,0:T(8,128)} %select_bitcast_fusion.1), custom_call_target="InvertDiagBlocksLowerTriangular" | custom-call | tf_op jit(solution)/shard_map/jit(cholesky)/cholesky | solution.py:49
  959.8 48.4 %custom-call.43 = f32[4,128,128]{2,1,0:T(8,128)} custom-call(f32[4,128,128]{2,1,0:T(8,128)} %convolution_subtract_fusion.35), custom_call_target="Cholesky" | custom-call | tf_op jit(solution)/shard_map/jit(cholesky)/cholesky | solution.py:49
  1012.4 6.8 while.18
  1019.1 80.4 %custom-call.45 = f32[4,2,128,128]{2,3,1,0:T(8,128)} custom-call(f32[4,2,128,128]{3,2,1,0:T(8,128)} %bitcast.807), custom_call_target="InvertDiagBlocksLowerTriangular" | custom-call | tf_op jit(solution)/shard_map/jit(_solve_triangular)/vmap()/triangular_solve | solution.py:52
  1122.2 46.9 %custom-call.46 = f32[4,128,128]{2,1,0:T(8,128)S(1)} custom-call(f32[4,128,128]{2,1,0:T(8,128)S(1)} %cholesky.359), custom_call_target="Cholesky" | custom-call | tf_op jit(solution)/shard_map/jit(cholesky)/cholesky | solution.py:49
  1172.3 40.8 %custom-call.47 = f32[4,1,128,128]{2,3,1,0:T(8,128)} custom-call(f32[4,1,128,128]{3,2,1,0:T(8,128)} %select_bitcast_fusion), custom_call_target="InvertDiagBlocksLowerTriangular" | custom-call | tf_op jit(solution)/shard_map/jit(cholesky)/cholesky | solution.py:49
  1216.8 48.4 %custom-call.48 = f32[4,128,128]{2,1,0:T(8,128)} custom-call(f32[4,128,128]{2,1,0:T(8,128)} %convolution_subtract_fusion.23), custom_call_target="Cholesky" | custom-call | tf_op jit(solution)/shard_map/jit(cholesky)/cholesky | solution.py:49
  1274.8 80.4 %custom-call.50 = f32[4,2,128,128]{2,3,1,0:T(8,128)} custom-call(f32[4,2,128,128]{3,2,1,0:T(8,128)} %bitcast.804), custom_call_target="InvertDiagBlocksLowerTriangular" | custom-call | tf_op jit(solution)/shard_map/jit(_solve_triangular)/vmap()/triangular_solve | solution.py:52
  1533.2 38.6 %psum.7 = f32[]{:T(128)} all-reduce(f32[]{:T(128)S(6)} %mul.209), channel_id=1, replica_groups=mesh['energy'=8,'mom'=4] {'energy','mom'}, use_global_device_ids=true, to_apply=%region_8.12 | all-reduce | flops 1 | bytes 8 | tf_op jit(solution)/shard_map/psum | solution.py:200
  (646 shorter events, 346.9 us)
Async XLA Ops:
  7.2 162.7 %all-reduce.10.cloned.1.call-start = ((), (), s32[]{:S(2)}) async-start(), calls=%async_computation.1 | async-start | bytes 8388608
  12.0 363.4 %all-gather.2.cloned.1.call-start = ((), (), s32[]{:S(2)}) async-start(), calls=%async_computation | async-start | bytes 5242880 | tf_op jit(solution)/shard_map/all_gather | solution.py:191
  172.5 24.6 %collective-permute-start.3 = (f32[2,4,1,2,128,128]{5,4,1,3,2,0:T(8,128)S(1)}, f32[2,4,1,2,128,128]{5,4,1,3,2,0:T(8,128)S(1)}, u32[]{:S(2)}, u32[]{:S(2)}) collective-permute-start(f32[2,4,1,2,128,128]{5,4,1,3,2,0:T(8,128)S(1)} %get-tuple-element.138), channel_id=1, source_target_pairs={{0,4},{4,8},{8,12},{12,16},{16,20},{20,24},{24,28},{28,0},{1,5},{5... | collective-permute-start | bytes 3145736 | tf_op jit(solution)/shard_map/ppermute | solution.py:20
  172.6 27.7 %collective-permute-start = (f32[2,4,1,2,128,128]{5,4,1,3,2,0:T(8,128)S(1)}, f32[2,4,1,2,128,128]{5,4,1,3,2,0:T(8,128)}, u32[]{:S(2)}, u32[]{:S(2)}) collective-permute-start(f32[2,4,1,2,128,128]{5,4,1,3,2,0:T(8,128)S(1)} %get-tuple-element.139), channel_id=1, source_target_pairs={{0,28},{4,0},{8,4},{12,8},{16,12},{20,16},{24,20},{28,24},{1,29},{... | collective-permute-start | bytes 3145736 | tf_op jit(solution)/shard_map/ppermute | solution.py:20
  198.4 27.1 %collective-permute-start.4 = (f32[2,4,1,2,128,128]{5,4,1,3,2,0:T(8,128)S(1)}, f32[2,4,1,2,128,128]{5,4,1,3,2,0:T(8,128)}, u32[]{:S(2)}, u32[]{:S(2)}) collective-permute-start(f32[2,4,1,2,128,128]{5,4,1,3,2,0:T(8,128)S(1)} %select_select_fusion.6), channel_id=1, source_target_pairs={{0,8},{4,12},{8,16},{12,20},{16,24},{20,28},{24,0},{28,4},{1,9},{5... | collective-permute-start | bytes 3145736 | tf_op jit(solution)/shard_map/ppermute | solution.py:20
  202.9 43.5 %collective-permute-start.1 = (f32[2,4,1,2,128,128]{5,4,1,3,2,0:T(8,128)S(1)}, f32[2,4,1,2,128,128]{5,4,1,3,2,0:T(8,128)}, u32[]{:S(2)}, u32[]{:S(2)}) collective-permute-start(f32[2,4,1,2,128,128]{5,4,1,3,2,0:T(8,128)S(1)} %select_select_fusion.9), channel_id=1, source_target_pairs={{0,24},{4,28},{8,0},{12,4},{16,8},{20,12},{24,16},{28,20},{1,25},{... | collective-permute-start | bytes 3145736 | tf_op jit(solution)/shard_map/ppermute | solution.py:20
  226.9 23.4 %collective-permute-start.5 = (f32[2,4,1,2,128,128]{5,4,1,3,2,0:T(8,128)S(1)}, f32[2,4,1,2,128,128]{5,4,1,3,2,0:T(8,128)}, u32[]{:S(2)}, u32[]{:S(2)}) collective-permute-start(f32[2,4,1,2,128,128]{5,4,1,3,2,0:T(8,128)S(1)} %select_select_fusion.5), channel_id=1, source_target_pairs={{0,16},{4,20},{8,24},{12,28},{16,0},{20,4},{24,8},{28,12},{1,17},{... | collective-permute-start | bytes 3145736 | tf_op jit(solution)/shard_map/ppermute | solution.py:20
  249.1 23.2 %collective-permute-start.2 = (f32[2,4,1,2,128,128]{5,4,1,3,2,0:T(8,128)S(1)}, f32[2,4,1,2,128,128]{5,4,1,3,2,0:T(8,128)S(1)}, u32[]{:S(2)}, u32[]{:S(2)}) collective-permute-start(f32[2,4,1,2,128,128]{5,4,1,3,2,0:T(8,128)S(1)} %select_select_fusion.8), channel_id=1, source_target_pairs={{0,16},{4,20},{8,24},{12,28},{16,0},{20,4},{24,8},{28,12},{1,17},{... | collective-permute-start | bytes 3145736 | tf_op jit(solution)/shard_map/ppermute | solution.py:20
  276.1 101.8 %copy-start.122 = (f32[4]{0:T(128)}, f32[4]{0:T(128)S(1)}, u32[]{:S(2)}) copy-start(f32[4]{0:T(128)S(1)} %multiply_add_fusion.3) | copy-start | bytes 52
  277.3 153.1 %copy-start.112 = (pred[128,128]{1,0:T(8,128)(4,1)}, pred[128,128]{1,0:T(8,128)(4,1)S(1)}, u32[]{:S(2)}) copy-start(pred[128,128]{1,0:T(8,128)(4,1)S(1)} %iota_compare_fusion.1) | copy-start | bytes 49156
  278.8 99.1 %copy-start.109 = (f32[128,128]{1,0:T(8,128)}, f32[128,128]{1,0:T(8,128)S(1)}, u32[]{:S(2)}) copy-start(f32[128,128]{1,0:T(8,128)S(1)} %get-tuple-element.184) | copy-start | bytes 196612
  759.9 85.1 %copy-start.44 = (f32[4,128,128]{2,1,0:T(8,128)S(1)}, f32[4,128,128]{2,1,0:T(8,128)}, u32[]{:S(2)}) copy-start(f32[4,128,128]{2,1,0:T(8,128)} %copy-done.43) | copy-start | bytes 786436
  759.9 86.8 %copy-start.62 = (f32[4,128,128]{2,1,0:T(8,128)S(1)}, f32[4,128,128]{2,1,0:T(8,128)}, u32[]{:S(2)}) copy-start(f32[4,128,128]{2,1,0:T(8,128)} %copy-done.61) | copy-start | bytes 786436
  865.2 49.3 %copy-start.113 = (pred[128,128]{1,0:T(8,128)(4,1)S(1)}, pred[128,128]{1,0:T(8,128)(4,1)}, u32[]{:S(2)}) copy-start(pred[128,128]{1,0:T(8,128)(4,1)} %copy-done.112) | copy-start | bytes 49156
  1011.5 89.7 %copy-start.64 = (f32[4,128,128]{2,1,0:T(8,128)S(1)}, f32[4,128,128]{2,1,0:T(8,128)}, u32[]{:S(2)}) copy-start(f32[4,128,128]{2,1,0:T(8,128)} %copy-done.63) | copy-start | bytes 786436
  1392.6 7.9 copy-start.23
  1407.9 7.2 copy-start.50
  1444.5 7.9 copy-start.65
  1466.4 7.0 copy-start.56
  1466.4 7.0 copy-start.77
  1466.4 7.0 copy-start.98
  1479.1 8.0 copy-start.48
  1496.4 8.0 copy-start.54
  1504.5 7.7 copy-start.52
  (116 other events, 403.0 us)
Sparse Core Ops, SparseCore 0:
  12.1 157.6 all-reduce.9
  275.5 99.8 all-gather.1
where the time goes:
time: 1590 us; the launch traced here: 1580 us
  other arithmetic  901 us (57%)
  waiting for transfers between devices  332 us (21%)
  matrix products  193 us (12%)
  local copies, waits for them, and re-layouts  83.7 us (5%)
  blocking collectives  38.6 us (2%)
  between operations  18.6 us (1%)
    another operation x34, other arithmetic, invert(): lower = jnp.linalg.cholesky(normal)  545 us
    another operation x10, other arithmetic, invert(): jax.scipy.linalg.solve_triangular(lower, middle, lower=True, trans=1)  323 us
    dot_general x188, matrix products, product(): return jnp.einsum('...ij,...jk->...ik', left, right, precision=precise)  160 us
    unnamed x3, waiting for transfers between devices  157 us
    all_gather x1, waiting for transfers between devices, shards(): lax.all_gather(jnp.stack([share_less, share_great], 0), 'mom', axis=2, ti...  96.6 us
    ppermute x6, waiting for transfers between devices, shifted(): lax.ppermute(array, axis, [(i, (i + by) % size) for i in range(size)])  78.8 us
    psum x1, blocking collectives, shards(): current = lax.psum(partial_flow, ('energy', 'mom'))  38.6 us
  transfers between devices with their start and end apart: 8, of which 6 were waited for; matrix products, arithmetic and copies ran while one was open for 1% of the time, Pallas kernels for 0%

commit v1 on v0

v1 whole, which is shorter than its diff:
```python
import functools
import math

import jax
import jax.numpy as jnp
from jax import lax
from jax.experimental import pallas as pl
from jax.experimental.pallas import tpu as pltpu
from jax.sharding import PartitionSpec as P

SMAX = 7

broaden = 0.2
contact_rate = 0.5
left_level = 0.3
right_level = -0.3
thermal = 0.1
band_edge = 2.0


def step_thresholds(count):
    bound = 1.0 - 3e-7
    out = [bound]
    for _ in range(count):
        root = math.sqrt(1.0 - bound)
        bound = (1.0 - root) / (1.0 + root)
        out.append(bound)
    return out


THRESHOLDS = step_thresholds(24)


def split(x):
    high = x.astype(jnp.bfloat16)
    low = (x - high.astype(jnp.float32)).astype(jnp.bfloat16)
    return high, low


def as_left(x):
    high, low = split(x)
    return jnp.concatenate([high, high, low], 1)


def as_right(x):
    width = x.shape[0]
    high, low = split(x)

    def block(t):
        return jnp.concatenate([t, jnp.concatenate([-t[:, width:], t[:, :width]], 1)], 0)

    wide = block(high)
    return jnp.concatenate([wide, block(low), wide], 0)


def mul(left, right):
    return jnp.dot(left, right, preferred_element_type=jnp.float32)


def dagger(x):
    width = x.shape[0]
    return jnp.concatenate([x[:, :width].T, -x[:, width:].T], 1)


def transport_kernel(
    scal, sig, ham, hop, less, great, flow, gr, gl, tg, tl, mat, mleft, cur, curl, cleft, cright
):
    count, slabs = less.shape[0], less.shape[1]
    width = less.shape[-1]
    row = lax.broadcasted_iota(jnp.int32, (width, width), 0)
    col = lax.broadcasted_iota(jnp.int32, (width, width), 1)
    eye = jnp.where(row == col, 1.0, 0.0).astype(jnp.float32)
    wrow = lax.broadcasted_iota(jnp.int32, (width, 2 * width), 0)
    wcol = lax.broadcasted_iota(jnp.int32, (width, 2 * width), 1)
    weye = jnp.where(wrow == wcol, 1.0, 0.0).astype(jnp.float32)

    def opened(packed):
        turned = packed.T
        imag = jnp.where(row >= col, packed, turned)
        real = jnp.where(row < col, packed, jnp.where(row > col, -turned, 0.0))
        return real, imag

    coup = jnp.concatenate([hop[0], hop[1]], 1)
    cleft[...] = as_left(coup)
    cright[...] = as_right(dagger(coup))

    def forward(s, carry):
        first = s == 0
        last = s == slabs - 1
        edge = jnp.where(jnp.logical_or(first, last), contact_rate, 0.0)
        for j in range(count):
            fill = jnp.where(first, scal[1, j], jnp.where(last, scal[2, j], 0.0))
            low = sig[0, j, s]
            d_re, d_im = opened(0.5 * (sig[1, j, s] - low))
            l_re, l_im = opened(low)
            mat[j, :, :width] = scal[0, j] * eye - ham[s, 0] - d_re
            mat[j, :, width:] = (broaden + edge) * eye - ham[s, 1] - d_im
            gl[s, j, :, :width] = l_re
            gl[s, j, :, width:] = l_im + (2.0 * contact_rate) * fill * eye

        @pl.when(s > 0)
        def _():
            for j in range(count):
                lead = mul(cleft[...], as_right(gr[s - 1, j]))
                tg[s - 1, j] = lead
                mat[j] = mat[j] - mul(as_left(lead), cright[...])
                lead = mul(cleft[...], as_right(gl[s - 1, j]))
                tl[s - 1, j] = lead
                gl[s, j] = gl[s, j] + mul(as_left(lead), cright[...])

        lower = None
        for j in range(count):
            m = mat[j]
            left = as_left(m)
            mleft[j] = left
            mh = dagger(m)
            norm = mul(left, as_right(mh))
            top = jnp.max(jnp.max(jnp.abs(norm), axis=1, keepdims=True), axis=0, keepdims=True)
            scaled = norm / top
            square = jnp.sum(jnp.sum(scaled * scaled, axis=1, keepdims=True), axis=0, keepdims=True)
            bound = top * jnp.sqrt(square) * 1.0001
            mat[j] = norm / bound
            cur[j] = mh / bound
            this = (0.98 * broaden * broaden) / bound
            lower = this if lower is None else jnp.minimum(lower, this)
        level = lower[0, 0]
        steps = jnp.int32(0)
        for threshold in THRESHOLDS[:-1]:
            steps = steps + jnp.where(level < threshold, 1, 0).astype(jnp.int32)
        lane = jnp.broadcast_to(lower, (1, 2 * width))

        def advance(j, prod, l):
            mu = 2.0 / (1.0 + l)
            gap = weye - mu * prod
            now = cur[j]
            cur[j] = mu * (now + mul(as_left(now), as_right(gap)))

        for j in range(count):
            advance(j, mat[j], lane)

        def newton(k, l):
            prods = [mul(mleft[j], as_right(cur[j])) for j in range(count)]
            for j in range(count):
                advance(j, prods[j], l)
            return jnp.minimum(4.0 * l / ((1.0 + l) * (1.0 + l)), 1.0)

        lane = jnp.minimum(4.0 * lane / ((1.0 + lane) * (1.0 + lane)), 1.0)
        lax.fori_loop(1, steps, newton, lane)
        for j in range(count):
            green = cur[j]
            gr[s, j] = green
            half = mul(as_left(green), as_right(gl[s, j]))
            gl[s, j] = mul(as_left(half), as_right(dagger(green)))
        return carry

    lax.fori_loop(0, slabs, forward, 0)

    def emit(s, j, full_r, full_l):
        l_re, l_im = full_l[:, :width], full_l[:, width:]
        r_re, r_im = full_r[:, :width], full_r[:, width:]
        less[j, s, 0] = l_re
        less[j, s, 1] = l_im
        great[j, s, 0] = l_re + r_re - r_re.T
        great[j, s, 1] = l_im + r_im + r_im.T

    for j in range(count):
        curl[j] = gl[slabs - 1, j]
        emit(slabs - 1, j, cur[j], curl[j])

    def backward(i, carry):
        s = slabs - 2 - i
        for j in range(count):
            green = gr[s, j]
            lead = mul(as_left(green), cright[...])
            uleft = as_left(lead)
            spread = as_left(mul(uleft, as_right(cur[j])))
            new_r = green + mul(spread, as_right(tg[s, j]))
            cross = mul(spread, as_right(tl[s, j]))
            inner = mul(as_left(mul(uleft, as_right(curl[j]))), as_right(dagger(lead)))
            new_l = gl[s, j] + inner + cross - dagger(cross)
            cur[j] = new_r
            curl[j] = new_l
            emit(s, j, new_r, new_l)
        return carry

    lax.fori_loop(0, slabs - 1, backward, 0)
    total = jnp.zeros((1, width), jnp.float32)
    for j in range(count):
        fill = scal[1, j]
        mix = fill * great[j, 0, 1] + (1.0 - fill) * less[j, 0, 1]
        total = total - jnp.sum(jnp.where(row == col, mix, 0.0), axis=0, keepdims=True)
    flow[...] = (2.0 * contact_rate) * total


def transport(scal, sig, ham, hop):
    count, slabs, width = sig.shape[1], sig.shape[2], sig.shape[-1]
    wide = (count, width, 2 * width)
    vmem = pl.BlockSpec(memory_space=pltpu.VMEM)
    block = jax.ShapeDtypeStruct((count, slabs, 2, width, width), jnp.float32)
    return pl.pallas_call(
        transport_kernel,
        out_shape=(block, block, jax.ShapeDtypeStruct((1, width), jnp.float32)),
        in_specs=[pl.BlockSpec(memory_space=pltpu.SMEM), vmem, vmem, vmem],
        out_specs=(vmem, vmem, vmem),
        scratch_shapes=[
            pltpu.VMEM((slabs,) + wide, jnp.float32),
            pltpu.VMEM((slabs,) + wide, jnp.float32),
            pltpu.VMEM((slabs,) + wide, jnp.float32),
            pltpu.VMEM((slabs,) + wide, jnp.float32),
            pltpu.VMEM(wide, jnp.float32),
            pltpu.VMEM((count, width, 6 * width), jnp.bfloat16),
            pltpu.VMEM(wide, jnp.float32),
            pltpu.VMEM(wide, jnp.float32),
            pltpu.VMEM((width, 6 * width), jnp.bfloat16),
            pltpu.VMEM((6 * width, 2 * width), jnp.bfloat16),
        ],
        compiler_params=pltpu.CompilerParams(vmem_limit_bytes=48 * 1024 * 1024),
        name="transport",
    )(scal, sig, ham, hop)


def rotated(array, axis, by):
    size = lax.axis_size(axis)
    if by % size == 0:
        return array
    return lax.ppermute(array, axis, [(i, (i + by) % size) for i in range(size)])


def moved(field, by):
    count = field.shape[1]
    by = max(-count, min(count, by))
    blank = jnp.zeros_like(field[:, : abs(by)])
    if by > 0:
        return jnp.concatenate([field[:, by:], blank], 1)
    if by < 0:
        return jnp.concatenate([blank, field[:, :by]], 1)
    return field


def exchanged(amount, mean):
    n_energy = lax.axis_size("energy")
    here = lax.axis_index("energy")
    turns, rest = divmod(amount, n_energy)
    above = rotated(mean, "energy", -rest)
    below = rotated(mean, "energy", rest)
    upper = jnp.where(here + rest >= n_energy, moved(above, turns + 1), moved(above, turns))
    under = jnp.where(here - rest < 0, moved(below, -turns - 1), moved(below, -turns))
    return upper, under


def shards(lesser, greater, hamiltonian, coupling, shift, phonon_weight):
    n_energy = lax.axis_size("energy")
    n_mom = lax.axis_size("mom")
    here = lax.axis_index("energy")
    mine = lax.axis_index("mom")
    per_dev, slabs, width = lesser.shape[0], lesser.shape[3], lesser.shape[-1]
    total = per_dev * n_energy
    part = slabs // n_mom
    row = lax.broadcasted_iota(jnp.int32, (width, width), 0)
    col = lax.broadcasted_iota(jnp.int32, (width, width), 1)

    def share(owner):
        def packed(x):
            x = lax.dynamic_slice_in_dim(x[:, 0, 0], owner * part, part, 1)
            return jnp.where(row >= col, x[:, :, 1], x[:, :, 0])

        return jnp.stack([packed(lesser), packed(greater)], 0)

    arrived = [
        rotated(share((mine + k) % n_mom), "mom", k) for k in range(1, n_mom)
    ]
    mean = share(mine)
    for piece in arrived:
        mean = mean + piece
    mean = mean / n_mom
    upper, beneath = lax.switch(
        jnp.clip(shift[0] - 1, 0, SMAX - 1),
        [functools.partial(exchanged, p) for p in range(1, SMAX + 1)],
        mean,
    )
    emission = phonon_weight[0]
    absorption = phonon_weight[1]
    own = jnp.stack(
        [
            emission * upper[0] + absorption * beneath[0],
            emission * beneath[1] + absorption * upper[1],
        ],
        0,
    )
    sig = jnp.zeros((2, per_dev, slabs, width, width), jnp.float32)
    sig = lax.dynamic_update_slice_in_dim(sig, own, mine * part, 2)
    for k in range(1, n_mom):
        piece = rotated(own, "mom", k)
        sig = lax.dynamic_update_slice_in_dim(sig, piece, ((mine - k) % n_mom) * part, 2)
    grid = (jnp.arange(per_dev) * n_energy + here).astype(jnp.float32)
    energy = (grid + 0.5) * (2.0 * band_edge / total) - band_edge
    scal = jnp.stack(
        [
            energy,
            jax.nn.sigmoid((left_level - energy) / thermal),
            jax.nn.sigmoid((right_level - energy) / thermal),
        ],
        0,
    )
    less_new, great_new, flowing = transport(scal, sig, hamiltonian[0], coupling[0])
    partial_flow = jnp.sum(flowing) * (2.0 * band_edge / total)
    current = lax.psum(partial_flow, ("energy", "mom"))
    return (less_new[:, None, None], great_new[:, None, None], current)


def solution(mesh):
    block = P(None, "energy", "mom", None, None, None, None)
    return jax.shard_map(
        shards,
        mesh=mesh,
        in_specs=(block, block, P("mom"), P("mom"), P(), P()),
        out_specs=(block, block, P()),
        check_vma=False,
    )
```

time: 1590 us -> 217 us (0.14)
  other arithmetic: 901 us -> 2.85 us
  waiting for transfers between devices: 332 us -> 83.5 us
  matrix products: 193 us -> 0 us
  local copies, waits for them, and re-layouts: 83.7 us -> 6.85 us
  Pallas kernels: 0 us -> 47.2 us
  between operations: 18.6 us -> 2.22 us
    another operation x62 -> x5, other arithmetic: 886 us -> 0.21 us  [the longest x3 0.11 us: share(): return jnp.stack([packed(lesser), packed(greater)], 0)]
    dot_general x188 -> x0, matrix products: 160 us -> none  [product(): return jnp.einsum('...ij,...jk->...ik', left, right, precision=precise)]
    unnamed x3 -> x0, waiting for transfers between devices: 157 us -> none
    all_gather x1 -> x0, waiting for transfers between devices: 96.6 us -> none  [shards(): lax.all_gather(jnp.stack([share_less, share_great], 0), 'mom', axis=2, ti...]
    pallas_call x0 -> x1, Pallas kernels: none -> 47.2 us  [transport(): pl.pallas_call(transport_kernel, out_shape=(block, block, jax.ShapeDtypeS...]
    another operation x44 -> x0, local copies, waits for them, and re-layouts: 34.3 us -> none  [the longest x29 24.2 us: invert(): jax.scipy.linalg.solve_triangular(lower, middle, lower=True, trans=1)]
    another operation x32 -> x0, matrix products: 33.3 us -> none  [the longest x12 14.3 us: invert(): middle = jax.scipy.linalg.solve_triangular(lower, rhs, lower=True)]
    unnamed x267 -> x6, local copies, waits for them, and re-layouts: 21.7 us -> 0.02 us
where the time goes in v1:
time: 217 us
  waiting for transfers between devices  83.5 us (38%)
  blocking collectives  49.8 us (23%)
  Pallas kernels  47.2 us (22%)
  starting transfers between devices  24.4 us (11%)
  local copies, waits for them, and re-layouts  6.85 us (3%)
  other arithmetic  2.85 us (1%)
  between operations  2.22 us (1%)
    ppermute x8, waiting for transfers between devices, rotated(): lax.ppermute(array, axis, [(i, (i + by) % size) for i in range(size)])  83.5 us
    psum x1, blocking collectives, shards(): current = lax.psum(partial_flow, ('energy', 'mom'))  49.8 us
    pallas_call x1, Pallas kernels, transport(): pl.pallas_call(transport_kernel, out_shape=(block, block, jax.ShapeDtypeS...  47.2 us
    ppermute x8, starting transfers between devices, rotated(): lax.ppermute(array, axis, [(i, (i + by) % size) for i in range(size)])  24.4 us
  transfers between devices with their start and end apart: 8, of which 6 were waited for; matrix products, arithmetic and copies ran while one was open for 1% of the time, Pallas kernels for 0%

profile of v1, /device:TPU:0, one launch (start us, length us, event | category | flops | bytes accessed | tf_op | source)
XLA Modules:
  0.0 216.9 jit_solution(7911007279894366406)
XLA Ops:
  0.7 2.4 %constant_dynamic-slice_fusion.6 = (f32[4,1,1,1,2,128,128]{6,5,4,3,2,1,0:T(8,128)S(1)}, f32[4,1,1,1,2,128,128]{6,5,4,3,2,1,0:T(8,128)S(1)}, f32[4,1,1,1,2,128,12...) fusion(f32[4,1,1,4,2,128,128]{6,5,4,3,2,1,0:T(8,128)} %param.14, ...), kind=kLoop, calls=%fused_computation.67 | loop fusion | bytes 8388624 | tf_op jit(solution)/shard_map/dynamic_slice | solution.py:264
  4.0 3.1 %collective-permute-start.13 = (f32[2,4,1,128,128]{4,3,2,1,0:T(8,128)S(1)}, f32[2,4,1,128,128]{4,3,2,1,0:T(8,128)S(1)}, u32[]{:S(2)}, u32[]{:S(2)}) collective-permute-start(f32[2,4,1,128,128]{4,3,2,1,0:T(8,128)S(1)} %pad_maximum_fusion), channel_id=1, source_target_pairs={{0,1},{1,2},{2,3},{3,0},{4,5},{5,6},{6,7},{7,4},{8,9},{9,10},{10,1... | collective-permute-start | bytes 1572872 | tf_op jit(solution)/shard_map/ppermute | solution.py:226
  7.1 2.7 %collective-permute-start.14 = (f32[2,4,1,128,128]{4,3,2,1,0:T(8,128)S(1)}, f32[2,4,1,128,128]{4,3,2,1,0:T(8,128)S(1)}, u32[]{:S(2)}, u32[]{:S(2)}) collective-permute-start(f32[2,4,1,128,128]{4,3,2,1,0:T(8,128)S(1)} %pad_maximum_fusion.1), channel_id=1, source_target_pairs={{0,2},{1,3},{2,0},{3,1},{4,6},{5,7},{6,4},{7,5},{8,10},{9,11},{10,... | collective-permute-start | bytes 1572872 | tf_op jit(solution)/shard_map/ppermute | solution.py:226
  9.8 1.4 collective-permute-start.15
  11.9 0.6 fusion.12
  12.5 9.6 %collective-permute-done.13 = f32[2,4,1,128,128]{4,3,2,1,0:T(8,128)S(1)} collective-permute-done((f32[2,4,1,128,128]{4,3,2,1,0:T(8,128)S(1)}, f32[2,4,1,128,128]{4,3,2,1,0:T(8,128)S(1)}, u32[]{:S(2)}, u32[]{:S(2)}) %collective-permute-start.13) | collective-permute-done | bytes 524320 | tf_op jit(solution)/shard_map/ppermute | solution.py:226
  22.0 21.6 %collective-permute-done.14 = f32[2,4,1,128,128]{4,3,2,1,0:T(8,128)S(1)} collective-permute-done((f32[2,4,1,128,128]{4,3,2,1,0:T(8,128)S(1)}, f32[2,4,1,128,128]{4,3,2,1,0:T(8,128)S(1)}, u32[]{:S(2)}, u32[]{:S(2)}) %collective-permute-start.14) | collective-permute-done | bytes 524320 | tf_op jit(solution)/shard_map/ppermute | solution.py:226
  43.8 26.2 %conditional.1 = (f32[2,4,1,128,128]{4,3,2,1,0:T(8,128)S(1)}, f32[2,4,1,128,128]{4,3,2,1,0:T(8,128)S(1)}) conditional(s32[]{:T(128)} %bitcast.1, f32[2,4,1,128,128]{4,3,2,1,0:T(8,128)S(1)} %fusion.2, f32[2,4,1,128,128]{4,3,2,1,0:T(8,128)S(1)} %fusion.2, f32[2,4,1,128,128]{4,3,2,1,0:T(8,128)S(1)} %fusion.2, ...), branch_computations={%region_0.1_spmd, %region_1.2_spmd, %region_2.3_spmd, %region_3.4_... | conditional | flops 262151 | bytes 8650924 | solution.py:276
  43.8 1.5 collective-permute-start.3
  45.3 1.4 collective-permute-start.2
  46.8 12.8 %collective-permute-done.3 = f32[2,4,1,128,128]{4,3,2,1,0:T(8,128)S(1)} collective-permute-done((f32[2,4,1,128,128]{4,3,2,1,0:T(8,128)S(1)}, f32[2,4,1,128,128]{4,3,2,1,0:T(8,128)S(1)}, u32[]{:S(2)}, u32[]{:S(2)}) %collective-permute-start.3) | collective-permute-done | bytes 524320 | tf_op jit(solution)/shard_map/cond/branch_1_fun/ppermute | solution.py:226
  59.6 10.2 %collective-permute-done.2 = f32[2,4,1,128,128]{4,3,2,1,0:T(8,128)S(1)} collective-permute-done((f32[2,4,1,128,128]{4,3,2,1,0:T(8,128)S(1)}, f32[2,4,1,128,128]{4,3,2,1,0:T(8,128)S(1)}, u32[]{:S(2)}, u32[]{:S(2)}) %collective-permute-start.2) | collective-permute-done | bytes 524320 | tf_op jit(solution)/shard_map/cond/branch_1_fun/ppermute | solution.py:226
  70.0 1.4 multiply_add_fusion.1
  71.7 11.8 %collective-permute-start.16 = (f32[2,4,1,128,128]{4,3,2,1,0:T(8,128)S(1)}, f32[2,4,1,128,128]{4,3,2,1,0:T(8,128)}, u32[]{:S(2)}, u32[]{:S(2)}) collective-permute-start(f32[2,4,1,128,128]{4,3,2,1,0:T(8,128)S(1)} %get-tuple-element.37), channel_id=1, source_target_pairs={{0,1},{1,2},{2,3},{3,0},{4,5},{5,6},{6,7},{7,4},{8,9},{9,10},{10,1... | collective-permute-start | bytes 1572872 | tf_op jit(solution)/shard_map/ppermute | solution.py:226
  83.5 0.6 collective-permute-start.17
  84.1 1.9 collective-permute-start.18
  86.0 10.5 %collective-permute-done.16 = f32[2,4,1,128,128]{4,3,2,1,0:T(8,128)} collective-permute-done((f32[2,4,1,128,128]{4,3,2,1,0:T(8,128)S(1)}, f32[2,4,1,128,128]{4,3,2,1,0:T(8,128)}, u32[]{:S(2)}, u32[]{:S(2)}) %collective-permute-start.16) | collective-permute-done | bytes 524320 | tf_op jit(solution)/shard_map/ppermute | solution.py:226
  96.5 1.1 constant_dynamic-update-slice_fusion.2
  97.6 18.8 %collective-permute-done.17 = f32[2,4,1,128,128]{4,3,2,1,0:T(8,128)} collective-permute-done((f32[2,4,1,128,128]{4,3,2,1,0:T(8,128)S(1)}, f32[2,4,1,128,128]{4,3,2,1,0:T(8,128)}, u32[]{:S(2)}, u32[]{:S(2)}) %collective-permute-start.17) | collective-permute-done | bytes 524320 | tf_op jit(solution)/shard_map/ppermute | solution.py:226
  116.4 1.1 constant_dynamic-update-slice_fusion.1
  117.5 1.1 constant_dynamic-update-slice_fusion.sig
  118.7 47.2 %transport.1 = (f32[4,4,2,128,128]{4,3,2,1,0:T(8,128)}, f32[4,4,2,128,128]{4,3,2,1,0:T(8,128)}, f32[1,128]{1,0:T(1,128)S(1)}) custom-call(f32[3,4]{1,0:T(4,128)S(1)} %pad_maximum_fusion.4.scal, f32[2,4,4,128,128]{4,3,2,1,0:T(8,128)S(1)} %constant_dynamic-update-slice_fusion.sig, f32[4,2,128,128]{3,2,1,0:T(8,128)S(1)} %bitcast.115, f32[2,128,128]{2,1,0:T(8,128)S(1)} %bitcast.116), custom_call_target="tpu_custom_call" | custom-call | tf_op jit(solution)/shard_map/transport/pallas_call | solution.py:200
  165.8 0.6 reduce_sum.9
  167.1 49.8 %psum.7 = f32[]{:T(128)} all-reduce(f32[]{:T(128)S(6)} %mul.79), channel_id=1, replica_groups=mesh['energy'=8,'mom'=4] {'energy','mom'}, use_global_device_ids=true, to_apply=%region_8.9 | all-reduce | flops 1 | bytes 8 | tf_op jit(solution)/shard_map/psum | solution.py:307
  (31 shorter events, 1.5 us)
Async XLA Ops:
  3.9 8.0 %copy-start.2 = (f32[2]{0:T(128)S(1)}, f32[2]{0:T(128)}, u32[]{:S(2)}) copy-start(f32[2]{0:T(128)} %param.18) | copy-start | bytes 28
  4.0 18.0 %collective-permute-start.13 = (f32[2,4,1,128,128]{4,3,2,1,0:T(8,128)S(1)}, f32[2,4,1,128,128]{4,3,2,1,0:T(8,128)S(1)}, u32[]{:S(2)}, u32[]{:S(2)}) collective-permute-start(f32[2,4,1,128,128]{4,3,2,1,0:T(8,128)S(1)} %pad_maximum_fusion), channel_id=1, source_target_pairs={{0,1},{1,2},{2,3},{3,0},{4,5},{5,6},{6,7},{7,4},{8,9},{9,10},{10,1... | collective-permute-start | bytes 1572872 | tf_op jit(solution)/shard_map/ppermute | solution.py:226
  7.1 36.5 %collective-permute-start.14 = (f32[2,4,1,128,128]{4,3,2,1,0:T(8,128)S(1)}, f32[2,4,1,128,128]{4,3,2,1,0:T(8,128)S(1)}, u32[]{:S(2)}, u32[]{:S(2)}) collective-permute-start(f32[2,4,1,128,128]{4,3,2,1,0:T(8,128)S(1)} %pad_maximum_fusion.1), channel_id=1, source_target_pairs={{0,2},{1,3},{2,0},{3,1},{4,6},{5,7},{6,4},{7,5},{8,10},{9,11},{10,... | collective-permute-start | bytes 1572872 | tf_op jit(solution)/shard_map/ppermute | solution.py:226
  9.8 33.8 %collective-permute-start.15 = (f32[2,4,1,128,128]{4,3,2,1,0:T(8,128)S(1)}, f32[2,4,1,128,128]{4,3,2,1,0:T(8,128)S(1)}, u32[]{:S(2)}, u32[]{:S(2)}) collective-permute-start(f32[2,4,1,128,128]{4,3,2,1,0:T(8,128)S(1)} %pad_maximum_fusion.2), channel_id=1, source_target_pairs={{0,3},{1,0},{2,1},{3,2},{4,7},{5,4},{6,5},{7,6},{8,11},{9,8},{10,9... | collective-permute-start | bytes 1572872 | tf_op jit(solution)/shard_map/ppermute | solution.py:226
  43.8 15.7 %collective-permute-start.3 = (f32[2,4,1,128,128]{4,3,2,1,0:T(8,128)S(1)}, f32[2,4,1,128,128]{4,3,2,1,0:T(8,128)S(1)}, u32[]{:S(2)}, u32[]{:S(2)}) collective-permute-start(f32[2,4,1,128,128]{4,3,2,1,0:T(8,128)S(1)} %param.1), channel_id=1, source_target_pairs={{0,8},{4,12},{8,16},{12,20},{16,24},{20,28},{24,0},{28,4},{1,9},{5... | collective-permute-start | bytes 1572872 | tf_op jit(solution)/shard_map/cond/branch_1_fun/ppermute | solution.py:226
  45.3 24.5 %collective-permute-start.2 = (f32[2,4,1,128,128]{4,3,2,1,0:T(8,128)S(1)}, f32[2,4,1,128,128]{4,3,2,1,0:T(8,128)S(1)}, u32[]{:S(2)}, u32[]{:S(2)}) collective-permute-start(f32[2,4,1,128,128]{4,3,2,1,0:T(8,128)S(1)} %param.1), channel_id=1, source_target_pairs={{0,24},{4,28},{8,0},{12,4},{16,8},{20,12},{24,16},{28,20},{1,25},{... | collective-permute-start | bytes 1572872 | tf_op jit(solution)/shard_map/cond/branch_1_fun/ppermute | solution.py:226
  71.6 47.1 %copy-start = (f32[1,4,2,128,128]{4,3,2,1,0:T(8,128)S(1)}, f32[1,4,2,128,128]{4,3,2,1,0:T(8,128)}, u32[]{:S(2)}) copy-start(f32[1,4,2,128,128]{4,3,2,1,0:T(8,128)} %param.15) | copy-start | bytes 1572868
  71.6 47.1 %copy-start.1 = (f32[1,2,128,128]{3,2,1,0:T(8,128)S(1)}, f32[1,2,128,128]{3,2,1,0:T(8,128)}, u32[]{:S(2)}) copy-start(f32[1,2,128,128]{3,2,1,0:T(8,128)} %param.16) | copy-start | bytes 393220
  71.7 24.9 %collective-permute-start.16 = (f32[2,4,1,128,128]{4,3,2,1,0:T(8,128)S(1)}, f32[2,4,1,128,128]{4,3,2,1,0:T(8,128)}, u32[]{:S(2)}, u32[]{:S(2)}) collective-permute-start(f32[2,4,1,128,128]{4,3,2,1,0:T(8,128)S(1)} %get-tuple-element.37), channel_id=1, source_target_pairs={{0,1},{1,2},{2,3},{3,0},{4,5},{5,6},{6,7},{7,4},{8,9},{9,10},{10,1... | collective-permute-start | bytes 1572872 | tf_op jit(solution)/shard_map/ppermute | solution.py:226
  83.5 32.9 %collective-permute-start.17 = (f32[2,4,1,128,128]{4,3,2,1,0:T(8,128)S(1)}, f32[2,4,1,128,128]{4,3,2,1,0:T(8,128)}, u32[]{:S(2)}, u32[]{:S(2)}) collective-permute-start(f32[2,4,1,128,128]{4,3,2,1,0:T(8,128)S(1)} %get-tuple-element.37), channel_id=1, source_target_pairs={{0,2},{1,3},{2,0},{3,1},{4,6},{5,7},{6,4},{7,5},{8,10},{9,11},{10,... | collective-permute-start | bytes 1572872 | tf_op jit(solution)/shard_map/ppermute | solution.py:226
  84.1 33.4 %collective-permute-start.18 = (f32[2,4,1,128,128]{4,3,2,1,0:T(8,128)S(1)}, f32[2,4,1,128,128]{4,3,2,1,0:T(8,128)}, u32[]{:S(2)}, u32[]{:S(2)}) collective-permute-start(f32[2,4,1,128,128]{4,3,2,1,0:T(8,128)S(1)} %get-tuple-element.37), channel_id=1, source_target_pairs={{0,3},{1,0},{2,1},{3,2},{4,7},{5,4},{6,5},{7,6},{8,11},{9,8},{10,9... | collective-permute-start | bytes 1572872 | tf_op jit(solution)/shard_map/ppermute | solution.py:226

commit v2 on v1

--- a/solution.py
+++ b/solution.py
@@ -7,6 +7,7 @@
 from jax.experimental import pallas as pl
 from jax.experimental.pallas import tpu as pltpu
 from jax.sharding import PartitionSpec as P
+
 
 SMAX = 7
 
@@ -63,7 +64,7 @@
 
 
 def transport_kernel(
-    scal, sig, ham, hop, less, great, flow, gr, gl, tg, tl, mat, mleft, cur, curl, cleft, cright
+    scal, sig_l, sig_g, ham, hop, less, great, flow, gr, gl, tg, tl, mat, mleft, cur, curl, cleft, cright
 ):
     count, slabs = less.shape[0], less.shape[1]
     width = less.shape[-1]
@@ -90,8 +91,8 @@
         edge = jnp.where(jnp.logical_or(first, last), contact_rate, 0.0)
         for j in range(count):
             fill = jnp.where(first, scal[1, j], jnp.where(last, scal[2, j], 0.0))
-            low = sig[0, j, s]
-            d_re, d_im = opened(0.5 * (sig[1, j, s] - low))
+            low = sig_l[j, s]
+            d_re, d_im = opened(0.5 * (sig_g[j, s] - low))
             l_re, l_im = opened(low)
             mat[j, :, :width] = scal[0, j] * eye - ham[s, 0] - d_re
             mat[j, :, width:] = (broaden + edge) * eye - ham[s, 1] - d_im
@@ -189,18 +190,18 @@
         fill = scal[1, j]
         mix = fill * great[j, 0, 1] + (1.0 - fill) * less[j, 0, 1]
         total = total - jnp.sum(jnp.where(row == col, mix, 0.0), axis=0, keepdims=True)
-    flow[...] = (2.0 * contact_rate) * total
-
-
-def transport(scal, sig, ham, hop):
-    count, slabs, width = sig.shape[1], sig.shape[2], sig.shape[-1]
+    flow[...] = jnp.broadcast_to((2.0 * contact_rate) * total, flow.shape)
+
+
+def transport(scal, sig_l, sig_g, ham, hop):
+    count, slabs, width = sig_l.shape[0], sig_l.shape[1], sig_l.shape[-1]
     wide = (count, width, 2 * width)
     vmem = pl.BlockSpec(memory_space=pltpu.VMEM)
     block = jax.ShapeDtypeStruct((count, slabs, 2, width, width), jnp.float32)
     return pl.pallas_call(
         transport_kernel,
-        out_shape=(block, block, jax.ShapeDtypeStruct((1, width), jnp.float32)),
-        in_specs=[pl.BlockSpec(memory_space=pltpu.SMEM), vmem, vmem, vmem],
+        out_shape=(block, block, jax.ShapeDtypeStruct((8, width), jnp.float32)),
+        in_specs=[pl.BlockSpec(memory_space=pltpu.SMEM), vmem, vmem, vmem, vmem],
         out_specs=(vmem, vmem, vmem),
         scratch_shapes=[
             pltpu.VMEM((slabs,) + wide, jnp.float32),
@@ -216,7 +217,70 @@
         ],
         compiler_params=pltpu.CompilerParams(vmem_limit_bytes=48 * 1024 * 1024),
         name="transport",
-    )(scal, sig, ham, hop)
+    )(scal, sig_l, sig_g, ham, hop)
+
+
+def sum_kernel(n_energy, n_mom, scale, flow, out, rows, table, local, send, recv):
+    here = lax.axis_index("energy")
+    mine = lax.axis_index("mom")
+    moms = [lax.rem(mine + k, n_mom) for k in range(1, n_mom)]
+    energies = [lax.rem(here + k, n_energy) for k in range(1, n_energy)]
+    barrier = pltpu.get_barrier_semaphore()
+    for m in moms:
+        pl.semaphore_signal(
+            barrier, inc=1, device_id=(here, m), device_id_type=pl.DeviceIdType.MESH
+        )
+    for e in energies:
+        pl.semaphore_signal(
+            barrier, inc=1, device_id=(e, mine), device_id_type=pl.DeviceIdType.MESH
+        )
+    pl.semaphore_wait(barrier, n_mom + n_energy - 2)
+
+    def spread(src, dst, base, devices):
+        copies = []
+        for k, device in enumerate(devices):
+            copy = pltpu.make_async_remote_copy(
+                src_ref=src,
+                dst_ref=dst,
+                send_sem=send.at[base + k],
+                recv_sem=recv.at[base + k],
+                device_id=device,
+                device_id_type=pl.DeviceIdType.MESH,
+            )
+            copy.start()
+            copies.append(copy)
+        own = pltpu.make_async_copy(src, dst, local)
+        own.start()
+        own.wait()
+        for copy in copies:
+            copy.wait()
+
+    spread(flow, rows.at[mine], 0, [(here, m) for m in moms])
+    spread(rows, table.at[here], n_mom - 1, [(e, mine) for e in energies])
+    total = jnp.sum(table[...].reshape(n_energy * n_mom * 8, -1), axis=0, keepdims=True)
+    total = jnp.sum(total, axis=1, keepdims=True) * (scale / 8.0)
+    out[...] = jnp.broadcast_to(total, out.shape)
+
+
+def summed(flow, scale):
+    n_energy, n_mom = lax.axis_size("energy"), lax.axis_size("mom")
+    copies = n_energy + n_mom - 2
+    vmem = pl.BlockSpec(memory_space=pltpu.VMEM)
+    return pl.pallas_call(
+        functools.partial(sum_kernel, n_energy, n_mom, scale),
+        out_shape=jax.ShapeDtypeStruct(flow.shape, jnp.float32),
+        in_specs=[vmem],
+        out_specs=vmem,
+        scratch_shapes=[
+            pltpu.VMEM((n_mom,) + flow.shape, jnp.float32),
+            pltpu.VMEM((n_energy, n_mom) + flow.shape, jnp.float32),
+            pltpu.SemaphoreType.DMA,
+            pltpu.SemaphoreType.DMA((copies,)),
+            pltpu.SemaphoreType.DMA((copies,)),
+        ],
+        compiler_params=pltpu.CompilerParams(collective_id=0, has_side_effects=True),
+        name="current_sum",
+    )(flow)[0, 0]
 
 
 def rotated(array, axis, by):
@@ -227,13 +291,13 @@
 
 
 def moved(field, by):
-    count = field.shape[1]
+    count = field.shape[0]
     by = max(-count, min(count, by))
-    blank = jnp.zeros_like(field[:, : abs(by)])
+    blank = jnp.zeros_like(field[: abs(by)])
     if by > 0:
-        return jnp.concatenate([field[:, by:], blank], 1)
+        return jnp.concatenate([field[by:], blank], 0)
     if by < 0:
-        return jnp.concatenate([blank, field[:, :by]], 1)
+        return jnp.concatenate([blank, field[:by]], 0)
     return field
 
 
@@ -259,39 +323,39 @@
     row = lax.broadcasted_iota(jnp.int32, (width, width), 0)
     col = lax.broadcasted_iota(jnp.int32, (width, width), 1)
 
-    def share(owner):
-        def packed(x):
-            x = lax.dynamic_slice_in_dim(x[:, 0, 0], owner * part, part, 1)
-            return jnp.where(row >= col, x[:, :, 1], x[:, :, 0])
-
-        return jnp.stack([packed(lesser), packed(greater)], 0)
-
-    arrived = [
-        rotated(share((mine + k) % n_mom), "mom", k) for k in range(1, n_mom)
-    ]
-    mean = share(mine)
-    for piece in arrived:
-        mean = mean + piece
-    mean = mean / n_mom
-    upper, beneath = lax.switch(
-        jnp.clip(shift[0] - 1, 0, SMAX - 1),
-        [functools.partial(exchanged, p) for p in range(1, SMAX + 1)],
-        mean,
-    )
-    emission = phonon_weight[0]
-    absorption = phonon_weight[1]
-    own = jnp.stack(
-        [
-            emission * upper[0] + absorption * beneath[0],
-            emission * beneath[1] + absorption * upper[1],
-        ],
-        0,
-    )
-    sig = jnp.zeros((2, per_dev, slabs, width, width), jnp.float32)
-    sig = lax.dynamic_update_slice_in_dim(sig, own, mine * part, 2)
-    for k in range(1, n_mom):
-        piece = rotated(own, "mom", k)
-        sig = lax.dynamic_update_slice_in_dim(sig, piece, ((mine - k) % n_mom) * part, 2)
+    def share(x, owner):
+        x = lax.dynamic_slice_in_dim(x[:, 0, 0], owner * part, part, 1)
+        return jnp.where(row >= col, x[:, :, 1], x[:, :, 0])
+
+    def reduced(x):
+        mean = share(x, mine)
+        for k in range(1, n_mom):
+            mean = mean + rotated(share(x, (mine + k) % n_mom), "mom", k)
+        return mean / n_mom
+
+    def scattered(mean, up_weight, down_weight):
+        upper, beneath = lax.switch(
+            jnp.clip(shift[0] - 1, 0, SMAX - 1),
+            [functools.partial(exchanged, p) for p in range(1, SMAX + 1)],
+            mean,
+        )
+        return up_weight * upper + down_weight * beneath
+
+    def gathered(own):
+        sig = jnp.zeros((per_dev, slabs, width, width), jnp.float32)
+        sig = lax.dynamic_update_slice_in_dim(sig, own, mine * part, 1)
+        for k in range(1, n_mom):
+            piece = rotated(own, "mom", k)
+            sig = lax.dynamic_update_slice_in_dim(sig, piece, ((mine - k) % n_mom) * part, 1)
+        return sig
+
+    mean_less = reduced(lesser)
+    mean_great = reduced(greater)
+    own_less = scattered(mean_less, phonon_weight[0], phonon_weight[1])
+    mean_great, own_less = lax.optimization_barrier((mean_great, own_less))
+    sig_less = gathered(own_less)
+    own_great = scattered(mean_great, phonon_weight[1], phonon_weight[0])
+    sig_great = gathered(own_great)
     grid = (jnp.arange(per_dev) * n_energy + here).astype(jnp.float32)
     energy = (grid + 0.5) * (2.0 * band_edge / total) - band_edge
     scal = jnp.stack(
@@ -302,9 +366,10 @@
         ],
         0,
     )
-    less_new, great_new, flowing = transport(scal, sig, hamiltonian[0], coupling[0])
-    partial_flow = jnp.sum(flowing) * (2.0 * band_edge / total)
-    current = lax.psum(partial_flow, ("energy", "mom"))
+    less_new, great_new, flowing = transport(
+        scal, sig_less, sig_great, hamiltonian[0], coupling[0]
+    )
+    current = summed(flowing, 2.0 * band_edge / total)
     return (less_new[:, None, None], great_new[:, None, None], current)
 
 

time: 217 us -> 179 us (0.82)
  blocking collectives: 49.8 us -> 0 us
  Pallas kernels: 47.2 us -> 63.1 us
  waiting for transfers between devices: 83.5 us -> 69.4 us
  starting transfers between devices: 24.4 us -> 33.1 us
    psum x1 -> x0, blocking collectives: 49.8 us -> none  [shards(): current = lax.psum(partial_flow, ('energy', 'mom'))]
    pallas_call x0 -> x1, Pallas kernels: none -> 15.9 us  [summed(): pl.pallas_call(functools.partial(sum_kernel, n_energy, n_mom, scale), out...]
    ppermute x8 -> x16, waiting for transfers between devices: 83.5 us -> 69.4 us  [rotated(): lax.ppermute(array, axis, [(i, (i + by) % size) for i in range(size)])]
    ppermute x8 -> x16, starting transfers between devices: 24.4 us -> 33.1 us  [rotated(): lax.ppermute(array, axis, [(i, (i + by) % size) for i in range(size)])]
    dynamic_update_slice x3 -> x7, local copies, waits for them, and re-layouts: 3.24 us -> 0.15 us  [the longest x6 0.13 us: gathered(): lax.dynamic_update_slice_in_dim(sig, piece, (mine - k) % n_mom * part, 1)]
  transfers between devices with their start and end apart: 8 -> 16, of which waited for: 6 -> 11; matrix products, arithmetic and copies ran while one was open for 1% -> 1% of each run, Pallas kernels for 0% -> 0%
where the time goes in v2:
time: 179 us; the launch traced here: 178 us
  waiting for transfers between devices  69.4 us (39%)
  Pallas kernels  63.1 us (35%)
  starting transfers between devices  33.1 us (18%)
  local copies, waits for them, and re-layouts  6.04 us (3%)
  other arithmetic  4.92 us (3%)
    ppermute x16, waiting for transfers between devices, rotated(): lax.ppermute(array, axis, [(i, (i + by) % size) for i in range(size)])  69.4 us
    pallas_call x1, Pallas kernels, transport(): pl.pallas_call(transport_kernel, out_shape=(block, block, jax.ShapeDtypeS...  47.2 us
    ppermute x16, starting transfers between devices, rotated(): lax.ppermute(array, axis, [(i, (i + by) % size) for i in range(size)])  33.1 us
    pallas_call x1, Pallas kernels, summed(): pl.pallas_call(functools.partial(sum_kernel, n_energy, n_mom, scale), out...  15.9 us
  transfers between devices with their start and end apart: 16, of which 11 were waited for; matrix products, arithmetic and copies ran while one was open for 1% of the time, Pallas kernels for 0%

profile of v2, /device:TPU:0, one launch (start us, length us, event | category | flops | bytes accessed | tf_op | source)
XLA Modules:
  0.0 178.3 jit_solution(17810992698083351814)
XLA Ops:
  0.7 2.4 %constant_dynamic-slice_fusion.3 = (f32[4,1,1,1,2,128,128]{6,5,4,3,2,1,0:T(8,128)S(1)}, f32[4,1,1,1,2,128,128]{6,5,4,3,2,1,0:T(8,128)S(1)}, f32[4,1,1,1,2,128,12...) fusion(f32[4,1,1,4,2,128,128]{6,5,4,3,2,1,0:T(8,128)} %param.20, ...), kind=kLoop, calls=%fused_computation.82 | loop fusion | bytes 8388624 | tf_op jit(solution)/shard_map/dynamic_slice | solution.py:327
  3.4 3.1 %collective-permute-start.29 = (f32[4,1,128,128]{3,2,1,0:T(8,128)S(1)}, f32[4,1,128,128]{3,2,1,0:T(8,128)}, u32[]{:S(2)}, u32[]{:S(2)}) collective-permute-start(f32[4,1,128,128]{3,2,1,0:T(8,128)S(1)} %get-tuple-element.60), channel_id=1, source_target_pairs={{0,1},{1,2},{2,3},{3,0},{4,5},{5,6},{6,7},{7,4},{8,9},{9,10},{10,1... | collective-permute-start | bytes 786440 | tf_op jit(solution)/shard_map/ppermute | solution.py:290
  6.5 2.6 %collective-permute-start.30 = (f32[4,1,128,128]{3,2,1,0:T(8,128)S(1)}, f32[4,1,128,128]{3,2,1,0:T(8,128)}, u32[]{:S(2)}, u32[]{:S(2)}) collective-permute-start(f32[4,1,128,128]{3,2,1,0:T(8,128)S(1)} %get-tuple-element.61), channel_id=1, source_target_pairs={{0,2},{1,3},{2,0},{3,1},{4,6},{5,7},{6,4},{7,5},{8,10},{9,11},{10,... | collective-permute-start | bytes 786440 | tf_op jit(solution)/shard_map/ppermute | solution.py:290
  9.1 1.3 collective-permute-start.31
  11.7 4.2 %collective-permute-done.29 = f32[4,1,128,128]{3,2,1,0:T(8,128)} collective-permute-done((f32[4,1,128,128]{3,2,1,0:T(8,128)S(1)}, f32[4,1,128,128]{3,2,1,0:T(8,128)}, u32[]{:S(2)}, u32[]{:S(2)}) %collective-permute-start.29) | collective-permute-done | bytes 262176 | tf_op jit(solution)/shard_map/ppermute | solution.py:290
  15.9 10.4 %collective-permute-done.30 = f32[4,1,128,128]{3,2,1,0:T(8,128)} collective-permute-done((f32[4,1,128,128]{3,2,1,0:T(8,128)S(1)}, f32[4,1,128,128]{3,2,1,0:T(8,128)}, u32[]{:S(2)}, u32[]{:S(2)}) %collective-permute-start.30) | collective-permute-done | bytes 262176 | tf_op jit(solution)/shard_map/ppermute | solution.py:290
  26.3 2.0 %fusion.7 = (f32[4,1,128,128]{3,2,1,0:T(8,128)}, f32[4,1,128,128]{3,2,1,0:T(8,128)S(1)}, f32[4,1,128,128]{3,2,1,0:T(8,128)S(1)}, f32[4,1,128,128]{3,2,1,0:T(8,128)S(1)}) fusion(f32[4,1,128,128]{3,2,1,0:T(8,128)} %collective-permute-done.31, f32[4,1,128,128]{3,2,1,0:T(8,128)} %collective-permute-done.30, f32[4,1,128,128]{3,2,1,0:T(8,128)} %collective-permute-done.29, ...), kind=kLoop, calls=%fused_computation.50 | loop fusion | flops 524288 | bytes 3948544 | tf_op jit(solution)/shard_map/div | solution.py:334
  28.3 6.1 %collective-permute-start.26 = (f32[4,1,128,128]{3,2,1,0:T(8,128)S(1)}, f32[4,1,128,128]{3,2,1,0:T(8,128)S(1)}, u32[]{:S(2)}, u32[]{:S(2)}) collective-permute-start(f32[4,1,128,128]{3,2,1,0:T(8,128)S(1)} %get-tuple-element.57), channel_id=1, source_target_pairs={{0,1},{1,2},{2,3},{3,0},{4,5},{5,6},{6,7},{7,4},{8,9},{9,10},{10,1... | collective-permute-start | bytes 786440 | tf_op jit(solution)/shard_map/ppermute | solution.py:290
  34.4 1.6 collective-permute-start.27
  37.4 10.9 %conditional.2 = (f32[4,1,128,128]{3,2,1,0:T(8,128)S(1)}, f32[4,1,128,128]{3,2,1,0:T(8,128)S(1)}) conditional(s32[]{:T(128)} %bitcast.17, f32[4,1,128,128]{3,2,1,0:T(8,128)} %get-tuple-element.56, f32[4,1,128,128]{3,2,1,0:T(8,128)} %get-tuple-element.56, f32[4,1,128,128]{3,2,1,0:T(8,128)} %get-tuple-element.56, ...), branch_computations={%region_0.1_spmd, %region_1.2_spmd, %region_2.3_spmd, %region_3.4_... | conditional | flops 131079 | bytes 4325548 | solution.py:337
  39.3 8.7 %collective-permute-done.5 = f32[4,1,128,128]{3,2,1,0:T(8,128)S(1)} collective-permute-done((f32[4,1,128,128]{3,2,1,0:T(8,128)}, f32[4,1,128,128]{3,2,1,0:T(8,128)S(1)}, u32[]{:S(2)}, u32[]{:S(2)}) %collective-permute-start.5) | collective-permute-done | bytes 262176 | tf_op jit(solution)/shard_map/cond/branch_2_fun/ppermute | solution.py:290
  49.7 2.5 %collective-permute-done.27 = f32[4,1,128,128]{3,2,1,0:T(8,128)S(1)} collective-permute-done((f32[4,1,128,128]{3,2,1,0:T(8,128)S(1)}, f32[4,1,128,128]{3,2,1,0:T(8,128)S(1)}, u32[]{:S(2)}, u32[]{:S(2)}) %collective-permute-start.27) | collective-permute-done | bytes 262176 | tf_op jit(solution)/shard_map/ppermute | solution.py:290
  52.3 10.6 %conditional.3 = (f32[4,1,128,128]{3,2,1,0:T(8,128)S(1)}, f32[4,1,128,128]{3,2,1,0:T(8,128)S(1)}) conditional(s32[]{:T(128)} %bitcast.17, f32[4,1,128,128]{3,2,1,0:T(8,128)S(1)} %fusion.15, f32[4,1,128,128]{3,2,1,0:T(8,128)S(1)} %fusion.15, f32[4,1,128,128]{3,2,1,0:T(8,128)S(1)} %fusion.15, ...), branch_computations={%region_7.8_spmd, %region_8.9_spmd, %region_9.10_spmd, %region_10.... | conditional | flops 131079 | bytes 4325548 | solution.py:337
  54.1 8.6 %collective-permute-done.17 = f32[4,1,128,128]{3,2,1,0:T(8,128)S(1)} collective-permute-done((f32[4,1,128,128]{3,2,1,0:T(8,128)S(1)}, f32[4,1,128,128]{3,2,1,0:T(8,128)S(1)}, u32[]{:S(2)}, u32[]{:S(2)}) %collective-permute-start.17) | collective-permute-done | bytes 262176 | tf_op jit(solution)/shard_map/cond/branch_2_fun/ppermute | solution.py:290
  64.3 6.1 %collective-permute-start.35 = (f32[4,1,128,128]{3,2,1,0:T(8,128)S(1)}, f32[4,1,128,128]{3,2,1,0:T(8,128)S(1)}, u32[]{:S(2)}, u32[]{:S(2)}) collective-permute-start(f32[4,1,128,128]{3,2,1,0:T(8,128)S(1)} %get-tuple-element.39), channel_id=1, source_target_pairs={{0,1},{1,2},{2,3},{3,0},{4,5},{5,6},{6,7},{7,4},{8,9},{9,10},{10,1... | collective-permute-start | bytes 786440 | tf_op jit(solution)/shard_map/ppermute | solution.py:290
  70.6 2.4 %collective-permute-start.36 = (f32[4,1,128,128]{3,2,1,0:T(8,128)S(1)}, f32[4,1,128,128]{3,2,1,0:T(8,128)S(1)}, u32[]{:S(2)}, u32[]{:S(2)}) collective-permute-start(f32[4,1,128,128]{3,2,1,0:T(8,128)S(1)} %get-tuple-element.39), channel_id=1, source_target_pairs={{0,2},{1,3},{2,0},{3,1},{4,6},{5,7},{6,4},{7,5},{8,10},{9,11},{10,... | collective-permute-start | bytes 786440 | tf_op jit(solution)/shard_map/ppermute | solution.py:290
  73.0 2.9 %collective-permute-start.37 = (f32[4,1,128,128]{3,2,1,0:T(8,128)S(1)}, f32[4,1,128,128]{3,2,1,0:T(8,128)S(1)}, u32[]{:S(2)}, u32[]{:S(2)}) collective-permute-start(f32[4,1,128,128]{3,2,1,0:T(8,128)S(1)} %get-tuple-element.39), channel_id=1, source_target_pairs={{0,3},{1,0},{2,1},{3,2},{4,7},{5,4},{6,5},{7,6},{8,11},{9,8},{10,9... | collective-permute-start | bytes 786440 | tf_op jit(solution)/shard_map/ppermute | solution.py:290
  76.6 2.9 %collective-permute-done.35 = f32[4,1,128,128]{3,2,1,0:T(8,128)S(1)} collective-permute-done((f32[4,1,128,128]{3,2,1,0:T(8,128)S(1)}, f32[4,1,128,128]{3,2,1,0:T(8,128)S(1)}, u32[]{:S(2)}, u32[]{:S(2)}) %collective-permute-start.35) | collective-permute-done | bytes 262176 | tf_op jit(solution)/shard_map/ppermute | solution.py:290
  79.5 1.9 %collective-permute-start.34 = (f32[4,1,128,128]{3,2,1,0:T(8,128)S(1)}, f32[4,1,128,128]{3,2,1,0:T(8,128)S(1)}, u32[]{:S(2)}, u32[]{:S(2)}) collective-permute-start(f32[4,1,128,128]{3,2,1,0:T(8,128)S(1)} %multiply_add_fusion.1), channel_id=1, source_target_pairs={{0,3},{1,0},{2,1},{3,2},{4,7},{5,4},{6,5},{7,6},{8,11},{9,8},{10,9... | collective-permute-start | bytes 786440 | tf_op jit(solution)/shard_map/ppermute | solution.py:290
  81.5 3.7 %collective-permute-done.32 = f32[4,1,128,128]{3,2,1,0:T(8,128)S(1)} collective-permute-done((f32[4,1,128,128]{3,2,1,0:T(8,128)S(1)}, f32[4,1,128,128]{3,2,1,0:T(8,128)S(1)}, u32[]{:S(2)}, u32[]{:S(2)}) %collective-permute-start.32) | collective-permute-done | bytes 262176 | tf_op jit(solution)/shard_map/ppermute | solution.py:290
  85.2 11.3 %collective-permute-done.36 = f32[4,1,128,128]{3,2,1,0:T(8,128)S(1)} collective-permute-done((f32[4,1,128,128]{3,2,1,0:T(8,128)S(1)}, f32[4,1,128,128]{3,2,1,0:T(8,128)S(1)}, u32[]{:S(2)}, u32[]{:S(2)}) %collective-permute-start.36) | collective-permute-done | bytes 262176 | tf_op jit(solution)/shard_map/ppermute | solution.py:290
  96.5 16.7 %collective-permute-done.33 = f32[4,1,128,128]{3,2,1,0:T(8,128)S(1)} collective-permute-done((f32[4,1,128,128]{3,2,1,0:T(8,128)S(1)}, f32[4,1,128,128]{3,2,1,0:T(8,128)S(1)}, u32[]{:S(2)}, u32[]{:S(2)}) %collective-permute-start.33) | collective-permute-done | bytes 262176 | tf_op jit(solution)/shard_map/ppermute | solution.py:290
  113.4 47.2 %transport.1 = (f32[4,4,2,128,128]{4,3,2,1,0:T(8,128)}, f32[4,4,2,128,128]{4,3,2,1,0:T(8,128)}, f32[8,128]{1,0:T(8,128)S(1)}) custom-call(f32[3,4]{1,0:T(4,128)S(1)} %pad_maximum_fusion.scal, f32[4,4,128,128]{3,2,1,0:T(8,128)S(1)} %constant_dynamic-update-slice_fusion.4.sig_l, f32[4,4,128,128]{3,2,1,0:T(8,128)S(1)} %constant_dynamic-update-slice_fusion.sig_g, ...), custom_call_target="tpu_custom_call" | custom-call | tf_op jit(solution)/shard_map/transport/pallas_call | solution.py:201
  161.2 15.9 %current_sum.1 = f32[8,128]{1,0:T(8,128)} custom-call(f32[8,128]{1,0:T(8,128)} %copy-done.2), custom_call_target="tpu_custom_call" | custom-call | tf_op jit(solution)/shard_map/current_sum/pallas_call | solution.py:269
  (57 shorter events, 12.0 us)
Async XLA Ops:
  3.4 12.5 %collective-permute-start.29 = (f32[4,1,128,128]{3,2,1,0:T(8,128)S(1)}, f32[4,1,128,128]{3,2,1,0:T(8,128)}, u32[]{:S(2)}, u32[]{:S(2)}) collective-permute-start(f32[4,1,128,128]{3,2,1,0:T(8,128)S(1)} %get-tuple-element.60), channel_id=1, source_target_pairs={{0,1},{1,2},{2,3},{3,0},{4,5},{5,6},{6,7},{7,4},{8,9},{9,10},{10,1... | collective-permute-start | bytes 786440 | tf_op jit(solution)/shard_map/ppermute | solution.py:290
  6.5 19.8 %collective-permute-start.30 = (f32[4,1,128,128]{3,2,1,0:T(8,128)S(1)}, f32[4,1,128,128]{3,2,1,0:T(8,128)}, u32[]{:S(2)}, u32[]{:S(2)}) collective-permute-start(f32[4,1,128,128]{3,2,1,0:T(8,128)S(1)} %get-tuple-element.61), channel_id=1, source_target_pairs={{0,2},{1,3},{2,0},{3,1},{4,6},{5,7},{6,4},{7,5},{8,10},{9,11},{10,... | collective-permute-start | bytes 786440 | tf_op jit(solution)/shard_map/ppermute | solution.py:290
  9.1 17.2 %collective-permute-start.31 = (f32[4,1,128,128]{3,2,1,0:T(8,128)S(1)}, f32[4,1,128,128]{3,2,1,0:T(8,128)}, u32[]{:S(2)}, u32[]{:S(2)}) collective-permute-start(f32[4,1,128,128]{3,2,1,0:T(8,128)S(1)} %get-tuple-element.62), channel_id=1, source_target_pairs={{0,3},{1,0},{2,1},{3,2},{4,7},{5,4},{6,5},{7,6},{8,11},{9,8},{10,9... | collective-permute-start | bytes 786440 | tf_op jit(solution)/shard_map/ppermute | solution.py:290
  10.4 0.7 copy-start.3
  28.3 21.5 %collective-permute-start.26 = (f32[4,1,128,128]{3,2,1,0:T(8,128)S(1)}, f32[4,1,128,128]{3,2,1,0:T(8,128)S(1)}, u32[]{:S(2)}, u32[]{:S(2)}) collective-permute-start(f32[4,1,128,128]{3,2,1,0:T(8,128)S(1)} %get-tuple-element.57), channel_id=1, source_target_pairs={{0,1},{1,2},{2,3},{3,0},{4,5},{5,6},{6,7},{7,4},{8,9},{9,10},{10,1... | collective-permute-start | bytes 786440 | tf_op jit(solution)/shard_map/ppermute | solution.py:290
  34.4 17.8 %collective-permute-start.27 = (f32[4,1,128,128]{3,2,1,0:T(8,128)S(1)}, f32[4,1,128,128]{3,2,1,0:T(8,128)S(1)}, u32[]{:S(2)}, u32[]{:S(2)}) collective-permute-start(f32[4,1,128,128]{3,2,1,0:T(8,128)S(1)} %get-tuple-element.58), channel_id=1, source_target_pairs={{0,2},{1,3},{2,0},{3,1},{4,6},{5,7},{6,4},{7,5},{8,10},{9,11},{10,... | collective-permute-start | bytes 786440 | tf_op jit(solution)/shard_map/ppermute | solution.py:290
  35.9 16.3 %collective-permute-start.28 = (f32[4,1,128,128]{3,2,1,0:T(8,128)S(1)}, f32[4,1,128,128]{3,2,1,0:T(8,128)S(1)}, u32[]{:S(2)}, u32[]{:S(2)}) collective-permute-start(f32[4,1,128,128]{3,2,1,0:T(8,128)S(1)} %get-tuple-element.59), channel_id=1, source_target_pairs={{0,3},{1,0},{2,1},{3,2},{4,7},{5,4},{6,5},{7,6},{8,11},{9,8},{10,9... | collective-permute-start | bytes 786440 | tf_op jit(solution)/shard_map/ppermute | solution.py:290
  37.5 10.5 %collective-permute-start.5 = (f32[4,1,128,128]{3,2,1,0:T(8,128)}, f32[4,1,128,128]{3,2,1,0:T(8,128)S(1)}, u32[]{:S(2)}, u32[]{:S(2)}) collective-permute-start(f32[4,1,128,128]{3,2,1,0:T(8,128)} %param.2), channel_id=1, source_target_pairs={{0,12},{4,16},{8,20},{12,24},{16,28},{20,0},{24,4},{28,8},{1,13},{... | collective-permute-start | bytes 786440 | tf_op jit(solution)/shard_map/cond/branch_2_fun/ppermute | solution.py:290
  38.1 10.2 %collective-permute-start.4 = (f32[4,1,128,128]{3,2,1,0:T(8,128)}, f32[4,1,128,128]{3,2,1,0:T(8,128)S(1)}, u32[]{:S(2)}, u32[]{:S(2)}) collective-permute-start(f32[4,1,128,128]{3,2,1,0:T(8,128)} %param.2), channel_id=1, source_target_pairs={{0,20},{4,24},{8,28},{12,0},{16,4},{20,8},{24,12},{28,16},{1,21},{... | collective-permute-start | bytes 786440 | tf_op jit(solution)/shard_map/cond/branch_2_fun/ppermute | solution.py:290
  52.3 10.4 %collective-permute-start.17 = (f32[4,1,128,128]{3,2,1,0:T(8,128)S(1)}, f32[4,1,128,128]{3,2,1,0:T(8,128)S(1)}, u32[]{:S(2)}, u32[]{:S(2)}) collective-permute-start(f32[4,1,128,128]{3,2,1,0:T(8,128)S(1)} %param.9), channel_id=1, source_target_pairs={{0,12},{4,16},{8,20},{12,24},{16,28},{20,0},{24,4},{28,8},{1,13},{... | collective-permute-start | bytes 786440 | tf_op jit(solution)/shard_map/cond/branch_2_fun/ppermute | solution.py:290
  53.4 9.4 %collective-permute-start.16 = (f32[4,1,128,128]{3,2,1,0:T(8,128)S(1)}, f32[4,1,128,128]{3,2,1,0:T(8,128)S(1)}, u32[]{:S(2)}, u32[]{:S(2)}) collective-permute-start(f32[4,1,128,128]{3,2,1,0:T(8,128)S(1)} %param.9), channel_id=1, source_target_pairs={{0,20},{4,24},{8,28},{12,0},{16,4},{20,8},{24,12},{28,16},{1,21},{... | collective-permute-start | bytes 786440 | tf_op jit(solution)/shard_map/cond/branch_2_fun/ppermute | solution.py:290
  64.3 15.2 %collective-permute-start.35 = (f32[4,1,128,128]{3,2,1,0:T(8,128)S(1)}, f32[4,1,128,128]{3,2,1,0:T(8,128)S(1)}, u32[]{:S(2)}, u32[]{:S(2)}) collective-permute-start(f32[4,1,128,128]{3,2,1,0:T(8,128)S(1)} %get-tuple-element.39), channel_id=1, source_target_pairs={{0,1},{1,2},{2,3},{3,0},{4,5},{5,6},{6,7},{7,4},{8,9},{9,10},{10,1... | collective-permute-start | bytes 786440 | tf_op jit(solution)/shard_map/ppermute | solution.py:290
  70.5 14.6 %collective-permute-start.32 = (f32[4,1,128,128]{3,2,1,0:T(8,128)S(1)}, f32[4,1,128,128]{3,2,1,0:T(8,128)S(1)}, u32[]{:S(2)}, u32[]{:S(2)}) collective-permute-start(f32[4,1,128,128]{3,2,1,0:T(8,128)S(1)} %multiply_add_fusion.1), channel_id=1, source_target_pairs={{0,1},{1,2},{2,3},{3,0},{4,5},{5,6},{6,7},{7,4},{8,9},{9,10},{10,1... | collective-permute-start | bytes 786440 | tf_op jit(solution)/shard_map/ppermute | solution.py:290
  70.6 25.9 %collective-permute-start.36 = (f32[4,1,128,128]{3,2,1,0:T(8,128)S(1)}, f32[4,1,128,128]{3,2,1,0:T(8,128)S(1)}, u32[]{:S(2)}, u32[]{:S(2)}) collective-permute-start(f32[4,1,128,128]{3,2,1,0:T(8,128)S(1)} %get-tuple-element.39), channel_id=1, source_target_pairs={{0,2},{1,3},{2,0},{3,1},{4,6},{5,7},{6,4},{7,5},{8,10},{9,11},{10,... | collective-permute-start | bytes 786440 | tf_op jit(solution)/shard_map/ppermute | solution.py:290
  73.0 40.2 %collective-permute-start.37 = (f32[4,1,128,128]{3,2,1,0:T(8,128)S(1)}, f32[4,1,128,128]{3,2,1,0:T(8,128)S(1)}, u32[]{:S(2)}, u32[]{:S(2)}) collective-permute-start(f32[4,1,128,128]{3,2,1,0:T(8,128)S(1)} %get-tuple-element.39), channel_id=1, source_target_pairs={{0,3},{1,0},{2,1},{3,2},{4,7},{5,4},{6,5},{7,6},{8,11},{9,8},{10,9... | collective-permute-start | bytes 786440 | tf_op jit(solution)/shard_map/ppermute | solution.py:290
  75.9 37.4 %collective-permute-start.33 = (f32[4,1,128,128]{3,2,1,0:T(8,128)S(1)}, f32[4,1,128,128]{3,2,1,0:T(8,128)S(1)}, u32[]{:S(2)}, u32[]{:S(2)}) collective-permute-start(f32[4,1,128,128]{3,2,1,0:T(8,128)S(1)} %multiply_add_fusion.1), channel_id=1, source_target_pairs={{0,2},{1,3},{2,0},{3,1},{4,6},{5,7},{6,4},{7,5},{8,10},{9,11},{10,... | collective-permute-start | bytes 786440 | tf_op jit(solution)/shard_map/ppermute | solution.py:290
  76.6 36.8 %copy-start = (f32[1,4,2,128,128]{4,3,2,1,0:T(8,128)S(1)}, f32[1,4,2,128,128]{4,3,2,1,0:T(8,128)}, u32[]{:S(2)}) copy-start(f32[1,4,2,128,128]{4,3,2,1,0:T(8,128)} %param.22) | copy-start | bytes 1572868
  76.6 36.8 %copy-start.1 = (f32[1,2,128,128]{3,2,1,0:T(8,128)S(1)}, f32[1,2,128,128]{3,2,1,0:T(8,128)}, u32[]{:S(2)}) copy-start(f32[1,2,128,128]{3,2,1,0:T(8,128)} %param.23) | copy-start | bytes 393220
  79.5 33.8 %collective-permute-start.34 = (f32[4,1,128,128]{3,2,1,0:T(8,128)S(1)}, f32[4,1,128,128]{3,2,1,0:T(8,128)S(1)}, u32[]{:S(2)}, u32[]{:S(2)}) collective-permute-start(f32[4,1,128,128]{3,2,1,0:T(8,128)S(1)} %multiply_add_fusion.1), channel_id=1, source_target_pairs={{0,3},{1,0},{2,1},{3,2},{4,7},{5,4},{6,5},{7,6},{8,11},{9,8},{10,9... | collective-permute-start | bytes 786440 | tf_op jit(solution)/shard_map/ppermute | solution.py:290
  160.6 0.6 copy-start.2
